TPU v7x, 128 devices: a whole 4x4x4 slice. The times are simulated.
128 devices in a mesh: row: 8 (over x, y_hi), col: 16 (over y_lo, z, core).
Axes of the slice: x: 4, y: 4 (y_hi: 2, y_lo: 2; y = y_hi * 2 + y_lo), z: 4, core: 2. Of those that a mesh axis runs over, the one named last changes fastest.
Arguments:
- b_values: bfloat16 [4096, 12288], P('row', 'col'), may hold values from -0.09375 to 0.09375
- tile_mask: int32 [16, 48], replicated, may hold values 0 or 1
Outputs:
- factored: float32 [12288, 12288], P('row', 'col')
Inputs may be any that keep to these rules, and one draw needn't show every extreme that they name: tile_mask[i, j] is 1 where tile (i, j) of B is kept and 0 where it is empty.
All inputs are finite; a program needn't handle non-finite values.
Results may differ from a plain program's by a relative error of at most 0.0017.
Values may be sent and summed in bfloat16 or wider, within the bound.
A program may use at most 128 MiB of HBM per device.

v0:
```python
import jax
import jax.numpy as jnp
from jax import lax
from jax.sharding import PartitionSpec as P

TILE = 256
PANEL = 512


def spread(block, axis, holder):
    block = jnp.where(lax.axis_index(axis) == holder, block, jnp.zeros_like(block))
    return lax.psum(block, axis)


def rows_for(lines, peers):
    spare = -lines.shape[0] % peers
    if not spare:
        return lines
    return jnp.concatenate([lines, jnp.zeros((spare, *lines.shape[1:]), lines.dtype)])


def broadcast_by_parts(x, axis, root):
    lines = jnp.where(lax.axis_index(axis) == root, x, jnp.zeros_like(x)).reshape(
        -1, *x.shape[1:][-1:]
    )
    padded = rows_for(lines, lax.axis_size(axis))
    own = lax.psum_scatter(padded, axis, scatter_dimension=0, tiled=True)
    return lax.all_gather(own, axis, axis=0, tiled=True)[: len(lines)].reshape(x.shape)


def from_root(x, axis, root):
    return lax.dynamic_index_in_dim(lax.all_gather(x, axis), root, 0, keepdims=False)


def expand_tiles(blocks):
    return jnp.repeat(jnp.repeat(blocks, TILE, axis=0), TILE, axis=1)


def factor_top(corner, panel):
    width = corner.shape[0]
    updated = corner
    factor = jnp.zeros_like(corner)
    for number in range(width // panel):
        lower_edge = number * panel
        upper_edge = lower_edge + panel
        diagonal_block = jnp.linalg.cholesky(updated[lower_edge:upper_edge, lower_edge:upper_edge])
        below = jax.scipy.linalg.solve_triangular(
            diagonal_block, updated[upper_edge:, lower_edge:upper_edge].T, lower=True
        ).T
        factor = factor.at[lower_edge:upper_edge, lower_edge:upper_edge].set(diagonal_block)
        factor = factor.at[upper_edge:, lower_edge:upper_edge].set(below)
        updated = updated.at[upper_edge:, upper_edge:].add(
            -jnp.dot(below, below.T, precision=lax.Precision.HIGHEST)
        )
    return factor


def panel_rows(source_rows, factor, panel):
    width = factor.shape[0]
    current = source_rows
    solved_parts = []
    for number in range(width // panel):
        lower_edge = number * panel
        upper_edge = lower_edge + panel
        solved = jax.scipy.linalg.solve_triangular(
            factor[lower_edge:upper_edge, lower_edge:upper_edge],
            current[:, lower_edge:upper_edge].T,
            lower=True,
        ).T
        solved_parts.append(solved)
        current = current.at[:, upper_edge:].add(
            -jnp.dot(
                solved,
                factor[upper_edge:, lower_edge:upper_edge].T,
                precision=lax.Precision.HIGHEST,
            )
        )
    return jnp.concatenate(solved_parts, axis=1)


def on_device(b_values, tile_mask):
    row_index = lax.axis_index("row")
    col_index = lax.axis_index("col")
    local_rows, width = b_values.shape
    height = 2 * width
    span = 2 * PANEL
    occupancy = lax.dynamic_slice(
        tile_mask,
        (row_index * (local_rows // TILE), col_index * (width // TILE)),
        (local_rows // TILE, width // TILE),
    )
    masked = b_values * expand_tiles(occupancy).astype(jnp.bfloat16)
    columns = lax.all_gather(masked, "row", axis=0, tiled=True)
    halves = []
    for offset in range(2):
        halves.append(spread(columns, "col", 2 * row_index + offset))
    left_factor = jnp.concatenate(halves, axis=1)
    product = lax.dot_general(
        left_factor, columns, (((0,), (0,)), ((), ())), preferred_element_type=jnp.float32
    )
    global_rows = row_index * height + lax.broadcasted_iota(jnp.int32, (height, width), 0)
    global_cols = col_index * width + lax.broadcasted_iota(jnp.int32, (height, width), 1)
    zeros = jnp.zeros((height, width), jnp.float32)
    system = product + jnp.where(global_rows == global_cols, 1.0, 0.0).astype(jnp.float32)
    strip_parts = []
    for owner in range(-(-span // width)):
        extent = min(width, span - owner * width)
        strip_parts.append(spread(system[:, :extent], "col", owner))
    strip = jnp.concatenate(strip_parts, axis=1)
    corner = broadcast_by_parts(strip[:span].astype(jnp.bfloat16), "row", 0).astype(jnp.float32)
    factor = factor_top(corner, PANEL)
    own_rows = panel_rows(strip, factor, PANEL)
    leading = from_root(system[:span].astype(jnp.bfloat16), "row", 0).astype(jnp.float32)
    other_rows = panel_rows(leading.T, factor, PANEL)
    trailing = system - jnp.dot(own_rows, other_rows.T, precision=lax.Precision.HIGHEST)
    padded = jnp.concatenate([own_rows, jnp.zeros((height, width), jnp.float32)], axis=1)
    lead_cols = lax.dynamic_slice_in_dim(padded, jnp.minimum(col_index * width, span), width, 1)
    return jnp.where(
        global_cols < span,
        jnp.where(global_rows >= global_cols, lead_cols, zeros),
        jnp.where(global_rows < span, zeros, trailing),
    )


def solution(mesh):
    return jax.shard_map(
        on_device,
        mesh=mesh,
        in_specs=(P("row", "col"), P()),
        out_specs=P("row", "col"),
        check_vma=False,
    )
```

profile of v0, /device:TPU:0, one launch (start us, length us, event | category | flops | bytes accessed | tf_op | source)
XLA Modules:
  0.0 990.1 jit_solution(9365573404130913296)
XLA Ops:
  9.9 100.8 %all-gather.5.cloned.1.call-done = bf16[4096,768]{0,1:T(8,128)(2,1)} async-done(((bf16[512,768]{0,1:T(8,128)(2,1)}), bf16[4096,768]{0,1:T(8,128)(2,1)}) %all-gather.5.cloned.1.call-update) | async-done | bytes 6291472 | tf_op jit(solution)/shard_map/all_gather | solution.py:93
  110.7 8.2 broadcast_select_fusion.1
  119.0 158.2 %all-reduce.8.cloned.1.call-done = (bf16[4096,768]{0,1:T(8,128)(2,1)}, bf16[4096,768]{0,1:T(8,128)(2,1)}) async-done(((bf16[4096,768]{0,1:T(8,128)(2,1)}, bf16[4096,768]{0,1:T(8,128)(2,1)}), (bf16[4096,768]{0,1:T(8,128)(2,1)}, bf16[4096,768]{0,1:T(8,128)(2,1)})) %all-reduce.8.cloned.1.call-update) | async-done | bytes 12582928 | tf_op jit(solution)/shard_map/psum | solution.py:12
  277.1 18.9 %broadcast_select_fusion.2 = (f32[1536,768]{1,0:T(8,128)}, f32[1536,768]{1,0:T(8,128)}) fusion(pred[]{:T(512)S(6)} %eq.19, s32[768]{0:T(1024)S(1)} %iota_add_fusion.1, s32[1536]{0:T(1024)S(1)} %iota_add_fusion, bf16[4096,768]{0,1:T(8,128)(2,1)} %all-gather.5.cloned.1.call-done, bf16[4096,768]{0,1:T(8,128)(2,1)} %get-tuple-element.138, ...), kind=kOutput, calls=%fused_computation.51 | convolution fusion | flops 9693560832 | bytes 28320768 | tf_op jit(solution)/shard_map/dot_general | solution.py:98
  298.8 136.1 %all-reduce.6.cloned.1.call-done = (f32[1536,768]{1,0:T(8,128)}, f32[1536,256]{1,0:T(8,128)}) async-done(((f32[1536,768]{1,0:T(8,128)}, f32[1536,256]{1,0:T(8,128)}), (f32[1536,768]{1,0:T(8,128)}, f32[1536,256]{1,0:T(8,128)})) %all-reduce.6.cloned.1.call-update) | async-done | bytes 6291472 | tf_op jit(solution)/shard_map/psum | solution.py:12
  442.6 76.8 %reduce-scatter.4.cloned.1.call-done = bf16[128,1024]{1,0:T(8,128)(2,1)} async-done(((bf16[1024,1024]{1,0:T(8,128)(2,1)}), bf16[128,1024]{1,0:T(8,128)(2,1)}) %reduce-scatter.4.cloned.1.call-update) | async-done | bytes 262160
  525.8 3.9 slice_bitcast_fusion
  529.7 47.5 %all-gather.7.cloned.1.call-done = bf16[1024,1024]{0,1:T(8,128)(2,1)} async-done(((bf16[128,1024]{0,1:T(8,128)(2,1)}), bf16[1024,1024]{0,1:T(8,128)(2,1)}) %all-gather.7.cloned.1.call-update) | async-done | bytes 2097168 | tf_op jit(solution)/shard_map/all_gather | solution.py:28
  583.8 11.7 %cholesky.286 = f32[128,128]{1,0:T(8,128)S(1)} custom-call(f32[128,128]{1,0:T(8,128)S(1)} %cholesky.426), custom_call_target="Cholesky" | custom-call | tf_op jit(solution)/shard_map/jit(cholesky)/cholesky | solution.py:46
  595.5 9.8 custom-call.36
  606.1 11.7 %cholesky.305 = f32[128,128]{1,0:T(8,128)S(1)} custom-call(f32[128,128]{1,0:T(8,128)S(1)} %cholesky.430), custom_call_target="Cholesky" | custom-call | tf_op jit(solution)/shard_map/jit(cholesky)/cholesky | solution.py:46
  617.9 10.3 %custom-call.37 = f32[1,128,128]{1,2,0:T(8,128)S(1)} custom-call(f32[1,128,128]{2,1,0:T(8,128)S(1)} %get-tuple-element.164), custom_call_target="InvertDiagBlocksLowerTriangular" | custom-call | tf_op jit(solution)/shard_map/jit(cholesky)/cholesky | solution.py:46
  628.8 11.7 %cholesky.326 = f32[128,128]{1,0:T(8,128)S(1)} custom-call(f32[128,128]{1,0:T(8,128)S(1)} %cholesky.435), custom_call_target="Cholesky" | custom-call | tf_op jit(solution)/shard_map/jit(cholesky)/cholesky | solution.py:46
  640.6 9.8 custom-call.38
  651.0 11.9 %cholesky.343 = f32[128,128]{1,0:T(8,128)S(1)} custom-call(f32[128,128]{1,0:T(8,128)S(1)} %convolution_subtract_fusion.20), custom_call_target="Cholesky" | custom-call | tf_op jit(solution)/shard_map/jit(cholesky)/cholesky | solution.py:46
  667.5 7.8 while.15
  675.3 39.3 %custom-call.39 = f32[4,128,128]{1,2,0:T(8,128)S(1)} custom-call(f32[4,128,128]{2,1,0:T(8,128)S(1)} %get-tuple-element.116), custom_call_target="InvertDiagBlocksLowerTriangular" | custom-call | tf_op jit(solution)/shard_map/jit(_solve_triangular)/triangular_solve | solution.py:65
  723.3 3.8 convolution_subtract_fusion.1
  744.5 11.7 %cholesky.358 = f32[128,128]{1,0:T(8,128)S(1)} custom-call(f32[128,128]{1,0:T(8,128)S(1)} %cholesky.439), custom_call_target="Cholesky" | custom-call | tf_op jit(solution)/shard_map/jit(cholesky)/cholesky | solution.py:46
  756.8 9.8 custom-call.40
  770.0 11.7 %cholesky.377 = f32[128,128]{1,0:T(8,128)S(1)} custom-call(f32[128,128]{1,0:T(8,128)S(1)} %cholesky.443), custom_call_target="Cholesky" | custom-call | tf_op jit(solution)/shard_map/jit(cholesky)/cholesky | solution.py:46
  782.2 9.9 %custom-call.41 = f32[1,128,128]{1,2,0:T(8,128)S(1)} custom-call(f32[1,128,128]{2,1,0:T(8,128)S(1)} %get-tuple-element.154), custom_call_target="InvertDiagBlocksLowerTriangular" | custom-call | tf_op jit(solution)/shard_map/jit(cholesky)/cholesky | solution.py:46
  795.3 13.2 %cholesky.398 = f32[128,128]{1,0:T(8,128)} custom-call(f32[128,128]{1,0:T(8,128)} %cholesky.448), custom_call_target="Cholesky" | custom-call | tf_op jit(solution)/shard_map/jit(cholesky)/cholesky | solution.py:46
  810.5 11.3 %custom-call.42 = f32[1,128,128]{1,2,0:T(8,128)} custom-call(f32[1,128,128]{2,1,0:T(8,128)} %get-tuple-element.151), custom_call_target="InvertDiagBlocksLowerTriangular" | custom-call | tf_op jit(solution)/shard_map/jit(cholesky)/cholesky | solution.py:46
  824.0 11.7 %cholesky.415 = f32[128,128]{1,0:T(8,128)S(1)} custom-call(f32[128,128]{1,0:T(8,128)S(1)} %convolution_subtract_fusion.19), custom_call_target="Cholesky" | custom-call | tf_op jit(solution)/shard_map/jit(cholesky)/cholesky | solution.py:46
  844.8 14.4 %while.16 = (s32[]{:T(128)}, f32[512,512]{1,0:T(8,128)}, s32[4,2]{0,1:T(2,128)S(1)}, f32[4,128,128]{2,1,0:T(8,128)}, s32[]{:T(128)}) while((s32[]{:T(128)}, f32[512,512]{1,0:T(8,128)}, s32[4,2]{0,1:T(2,128)S(1)}, f32[4,128,128]{2,1,0:T(8,128)}, s32[]{:T(128)}) %tuple.109), condition=%wide.while_cond.6.clone, body=%wide.while_body.6.clone.sunk | while | flops 2 | bytes 132205 | solution.py:65
  859.2 41.1 %custom-call.43 = f32[4,128,128]{1,2,0:T(8,128)} custom-call(f32[4,128,128]{2,1,0:T(8,128)} %get-tuple-element.117), custom_call_target="InvertDiagBlocksLowerTriangular" | custom-call | tf_op jit(solution)/shard_map/jit(_solve_triangular)/triangular_solve | solution.py:65
  900.4 5.4 convolution_subtract_fusion.4
  907.5 7.8 fusion.17
  925.6 3.8 convolution_subtract_fusion
  932.2 5.3 convolution_subtract_fusion.2
  963.9 18.9 %fusion.11 = f32[1536,768]{1,0:T(8,128)} fusion(f32[1536,768]{1,0:T(8,128)S(1)} %broadcast_in_dim.25, s32[]{:T(128)S(6)} %select_n.79, f32[1536,512]{1,0:T(8,128)S(1)} %copy-done.19, f32[1536,512]{1,0:T(8,128)S(1)} %copy-done.20, f32[1536,768]{1,0:T(8,128)S(1)} %bitcast.177, f32[768,512]{0,1:T(8,128)S(1)} %maximum_bitcast_fusion.1, ...), kind=kOutput, calls=%fused_computation.20 | convolution fusion | flops 14506131456 | bytes 29899780 | tf_op jit(solution)/shard_map/dot_general | solution.py:115
  (233 shorter events, 137.8 us)
Async XLA Ops:
  6.5 104.2 %all-gather.5.cloned.1.call-start = ((), (), s32[]{:S(2)}) async-start(), calls=%async_computation.1 | async-start | bytes 7077888 | tf_op jit(solution)/shard_map/all_gather | solution.py:93
  9.9 267.3 %all-reduce.8.cloned.1.call-start = ((), (), s32[]{:S(2)}) async-start(), calls=%async_computation.6 | async-start | bytes 25165824 | tf_op jit(solution)/shard_map/psum | solution.py:12
  118.9 316.1 %all-reduce.6.cloned.1.call-start = ((), (), s32[]{:S(2)}) async-start(), calls=%async_computation.5 | async-start | bytes 12582912 | tf_op jit(solution)/shard_map/psum | solution.py:12
  298.8 220.7 %reduce-scatter.4.cloned.1.call-start = ((), (), s32[]{:S(2)}) async-start(), calls=%async_computation.4 | async-start | bytes 2359296
  435.0 3.2 copy-start.29
  442.5 134.7 %all-gather.7.cloned.1.call-start = ((), (), s32[]{:S(2)}) async-start(), calls=%async_computation.2 | async-start | bytes 2359296 | tf_op jit(solution)/shard_map/all_gather | solution.py:28
  521.2 422.6 %all-gather.9.cloned.1.call-start = ((), (), s32[]{:S(2)}) async-start(), calls=%async_computation.3 | async-start | bytes 14155776 | tf_op jit(solution)/shard_map/all_gather | solution.py:32
  577.2 3.9 copy-start.2
  675.3 60.1 %copy-start.3 = (f32[512,512]{1,0:T(8,128)}, f32[512,512]{1,0:T(8,128)S(1)}, u32[]{:S(2)}) copy-start(f32[512,512]{1,0:T(8,128)S(1)} %get-tuple-element.289) | copy-start | bytes 3145732
  714.7 3.2 copy-start.23
  730.0 4.1 copy-start.24
  732.3 4.2 copy-start.5
  844.8 62.6 %copy-start.6 = (f32[128,512]{1,0:T(8,128)S(1)}, f32[128,512]{1,0:T(8,128)}, u32[]{:S(2)}) copy-start(f32[128,512]{1,0:T(8,128)} %copy-done.5) | copy-start | bytes 786436
  844.8 62.6 %copy-start.8 = (f32[128,1536]{0,1:T(8,128)S(1)}, f32[128,1536]{0,1:T(8,128)}, u32[]{:S(2)}) copy-start(f32[128,1536]{0,1:T(8,128)} %copy.28) | copy-start | bytes 2359300
  900.3 7.1 copy-start.10
  900.3 7.1 copy-start.12
  900.4 7.1 copy-start.27
  900.4 7.1 copy-start.31
  900.4 7.1 copy-start.36
  907.5 7.8 copy-start.14
  917.0 3.0 copy-start.4
  932.2 7.0 copy-start.9
  932.2 7.0 copy-start.11
  932.2 7.0 copy-start.13
  932.2 7.0 copy-start.15
  939.2 2.7 copy-start.18
  951.2 10.3 %slice-start = ((s8[4718592]{0:T(1024)(128)(4,1)}), s8[4194304]{0:T(1024)(128)(4,1)S(1)}, s32[]{:S(2)}) async-start(s8[4718592]{0:T(1024)(128)(4,1)} %bitcast.176), calls=%async_computation.7 | async-start | bytes 8388608
  953.9 3.1 copy-start.33
  957.5 4.0 slice-start.1
  961.2 2.8 copy-start.19
  961.2 2.7 copy-start.38
  961.2 2.7 copy-start.39
  (16 other events, 29.0 us)
Sparse Core Ops, SparseCore 0:
  10.0 100.6 all-gather.4
  119.0 158.0 all-reduce.7
  298.9 136.0 all-reduce.5
  442.7 76.7 reduce-scatter.3
  521.5 55.6 all-gather.6
  579.4 145.7 all-gather.8
where the time goes:
time: 998 us; the launch traced here: 990 us
  waiting for transfers between devices  519 us (52%)
  other arithmetic  271 us (27%)
  matrix products  113 us (11%)
  local copies, waits for them, and re-layouts  65.9 us (7%)
  between operations  20.2 us (2%)
    psum x2, waiting for transfers between devices, spread(): return lax.psum(block, axis)  294 us
    another operation x29, other arithmetic, factor_top(): jnp.linalg.cholesky(updated[lower_edge:upper_edge, lower_edge:upper_edge])  166 us
    all_gather x1, waiting for transfers between devices, on_device(): columns = lax.all_gather(masked, 'row', axis=0, tiled=True)  101 us
    another operation x5, other arithmetic, panel_rows(): jax.scipy.linalg.solve_triangular(factor[lower_edge:upper_edge, lower_edg...  81.7 us
    unnamed x7, waiting for transfers between devices  76.9 us
    another operation x28, matrix products, panel_rows(): jax.scipy.linalg.solve_triangular(factor[lower_edge:upper_edge, lower_edg...  48.5 us
    all_gather x1, waiting for transfers between devices, broadcast_by_parts(): lax.all_gather(own, axis, axis=0, tiled=True)[:len(lines)].reshape(x.shape)  47.5 us
    another operation x33, local copies, waits for them, and re-layouts, panel_rows(): jax.scipy.linalg.solve_triangular(factor[lower_edge:upper_edge, lower_edg...  29.9 us
  transfers between devices with their start and end apart: 6, of which 5 were waited for; matrix products, arithmetic and copies ran while one was open for 37% of the time, Pallas kernels for 0%

commit v1 on v0

v1 whole, which is shorter than its diff:
```python
import functools

import jax
import jax.numpy as jnp
from jax import lax
from jax.experimental import pallas as pl
from jax.experimental.pallas import tpu as pltpu
from jax.sharding import PartitionSpec as P

TILE = 256
PANEL = 512
SPAN = 2 * PANEL
NB = 128
BLOCKS = SPAN // NB
MESH = pl.DeviceIdType.MESH
HIGHEST = lax.Precision.HIGHEST
VMEM_LIMIT = 66_000_000


def nn(a, b):
    return lax.dot_general(a, b, (((1,), (0,)), ((), ())), preferred_element_type=jnp.float32)


def nt(a, b):
    return lax.dot_general(a, b, (((1,), (1,)), ((), ())), preferred_element_type=jnp.float32)


def nn_hi(a, b):
    return lax.dot_general(
        a, b, (((1,), (0,)), ((), ())), precision=HIGHEST, preferred_element_type=jnp.float32
    )


def nt_hi(a, b):
    return lax.dot_general(
        a, b, (((1,), (1,)), ((), ())), precision=HIGHEST, preferred_element_type=jnp.float32
    )


def tn_hi(a, b):
    return lax.dot_general(
        a, b, (((0,), (0,)), ((), ())), precision=HIGHEST, preferred_element_type=jnp.float32
    )


class Stream:
    def __init__(self, index, send, recv, slot, device, u, v):
        self.index, self.send, self.recv = index, send, recv
        self.slot, self.device, self.u, self.v = slot, device, u, v
        self.sent = []

    def _at(self, du, dv):
        return lax.rem(self.u + du + 4, 4), (self.v if dv == 0 else 1 - self.v)

    def _copy(self, label, ref, du, dv):
        uu, vv = self._at(du, dv)
        return pltpu.make_async_remote_copy(
            src_ref=ref,
            dst_ref=ref,
            send_sem=self.send.at[self.index, label],
            recv_sem=self.recv.at[self.index, label],
            device_id=self.device(uu, vv),
            device_id_type=MESH,
        )

    def push(self, label, block, half, to):
        copy = self._copy(label, self.slot(*self._at(*block), half), *to)
        copy.start()
        self.sent.append(copy)

    def arrived(self, label, block, half, source):
        self._copy(label, self.slot(*self._at(*block), half), *source).wait_recv()

    def send_own(self):
        self.push(0, (0, 0), None, (0, 1))
        self.push(1, (0, 0), None, (1, 0))
        self.push(2, (0, 0), None, (-1, 0))

    def send_pair(self):
        self.arrived(0, (0, 1), None, (0, 1))
        self.push(3, (0, 1), None, (1, 0))
        self.push(4, (0, 1), None, (-1, 0))

    def relay_own(self):
        self.arrived(1, (-1, 0), None, (-1, 0))
        self.push(5, (-1, 0), 0, (1, 0))
        self.arrived(2, (1, 0), None, (1, 0))
        self.push(6, (1, 0), 1, (-1, 0))

    def relay_pair(self):
        self.arrived(3, (-1, 1), None, (-1, 0))
        self.push(7, (-1, 1), 0, (1, 0))
        self.arrived(4, (1, 1), None, (1, 0))
        self.push(8, (1, 1), 1, (-1, 0))

    def end_own(self):
        self.arrived(5, (2, 0), 0, (-1, 0))
        self.arrived(6, (2, 0), 1, (1, 0))

    def end_pair(self):
        self.arrived(7, (2, 1), 0, (-1, 0))
        self.arrived(8, (2, 1), 1, (1, 0))

    def drain(self):
        for copy in self.sent:
            copy.wait_send()


def gather_kernel(
    m_ref, mt_ref, c_ref, a_ref, sq_ref, sr_ref,
    left, right, b1t, send, recv, swap_send, swap_recv, one_send, one_recv, local,
):
    row, col = lax.axis_index("row"), lax.axis_index("col")
    x, yh = lax.div(row, 2), lax.rem(row, 2)
    core, q = lax.rem(col, 2), lax.div(col, 2)
    yl, z = lax.div(q, 4), lax.rem(q, 4)
    depth, width = m_ref.shape
    height = 2 * width
    piece = SPAN // 2
    other = (row, q * 2 + 1 - core)

    def over_row(u, v):
        return (2 * u + v, col)

    def over_col(u, v):
        return (row, (4 * v + u) * 2 + core)

    def part(start, size, half):
        if half is None:
            return pl.ds(pl.multiple_of(start, 128), size)
        return pl.ds(pl.multiple_of(start + half * (size // 2), 128), size // 2)

    def right_slot(u, v, half):
        return right.at[2 * u + v, part(0, depth, half), :]

    def left_slot(u, v, half):
        return left.at[4 * v + u, part(core * width, width, half), :]

    def b1_slot(u, v, half):
        return b1t.at[2 * u + v, part(core * piece, piece, half), :]

    r_stream = Stream(0, send, recv, right_slot, over_row, x, yh)
    b_stream = Stream(1, send, recv, b1_slot, over_row, x, yh)
    l_stream = Stream(2, send, recv, left_slot, over_col, z, yl)
    swaps = []

    def swap(base, number, ref):
        copy = pltpu.make_async_remote_copy(
            src_ref=ref, dst_ref=ref,
            send_sem=swap_send.at[base + number], recv_sem=swap_recv.at[base + number],
            device_id=other, device_id_type=MESH,
        )
        copy.start()
        swaps.append(copy)

    def single(number, ref, target, place=None):
        return pltpu.make_async_remote_copy(
            src_ref=ref, dst_ref=ref if place is None else place,
            send_sem=one_send.at[number], recv_sem=one_recv.at[number],
            device_id=target, device_id_type=MESH,
        )

    own_right = pltpu.make_async_copy(m_ref, right.at[row], local.at[0])
    own_right.start()

    barrier = pltpu.get_barrier_semaphore()
    mirror = (q, 2 * row + core)
    friends = [
        over_row(lax.rem(x + 1, 4), yh), over_row(lax.rem(x + 3, 4), yh), over_row(x, 1 - yh),
        over_col(lax.rem(z + 1, 4), yl), over_col(lax.rem(z + 3, 4), yl), over_col(z, 1 - yl),
        other,
    ]
    for friend in friends:
        pl.semaphore_signal(barrier, inc=1, device_id=friend, device_id_type=MESH)

    @pl.when(row != q)
    def _():
        pl.semaphore_signal(barrier, inc=1, device_id=mirror, device_id_type=MESH)
        pl.semaphore_wait(barrier, len(friends) + 1)

    @pl.when(row == q)
    def _():
        pl.semaphore_wait(barrier, len(friends))

    mine = part(core * width, width, None)

    @pl.when(row != q)
    def _():
        single(0, mt_ref, mirror, left.at[row, mine, :]).start()

    @pl.when(row == q)
    def _():
        pltpu.make_async_copy(mt_ref, left.at[row, mine, :], local.at[1]).start()

    seed = jnp.logical_and(yl == 0, z == 0)
    spare = b1t.at[row, pl.ds(piece, width - piece), :]
    low = b1t.at[row, pl.ds(0, piece), :]
    high = b1t.at[row, pl.ds(width, SPAN - width), :]
    own_piece = b1_slot(x, yh, None)

    def to_col(zz, yy):
        return over_col(zz, yy)

    @pl.when(jnp.logical_and(seed, core == 0))
    def _():
        single(1, mt_ref.at[pl.ds(piece, width - piece), :], other, spare).start()
        copy = pltpu.make_async_copy(mt_ref.at[pl.ds(0, piece), :], low, local.at[2])
        copy.start()
        copy.wait()

    @pl.when(jnp.logical_and(seed, core == 1))
    def _():
        copy = pltpu.make_async_copy(mt_ref.at[pl.ds(0, SPAN - width), :], high, local.at[2])
        copy.start()
        copy.wait()
        single(1, spare, other).wait_recv()

    @pl.when(seed)
    def _():
        single(2, own_piece, to_col(0, 1)).start()
        single(3, own_piece, to_col(1, 0)).start()
        single(4, own_piece, to_col(3, 0)).start()

    own_right.wait()
    r_stream.send_own()

    @pl.when(row != q)
    def _():
        single(0, mt_ref, mirror, left.at[q, mine, :]).wait()

    @pl.when(row == q)
    def _():
        pltpu.make_async_copy(mt_ref, left.at[row, mine, :], local.at[1]).wait()

    l_stream.send_own()
    swap(0, 0, left_slot(z, yl, None))

    @pl.when(jnp.logical_and(z == 0, yl == 1))
    def _():
        single(2, own_piece, to_col(0, 0)).wait_recv()
        single(3, own_piece, to_col(1, 1)).start()
        single(4, own_piece, to_col(3, 1)).start()

    @pl.when(z == 1)
    def _():
        single(3, own_piece, to_col(0, yl)).wait_recv()
        single(5, b1_slot(x, yh, 0), to_col(2, yl)).start()

    @pl.when(z == 3)
    def _():
        single(4, own_piece, to_col(0, yl)).wait_recv()
        single(6, b1_slot(x, yh, 1), to_col(2, yl)).start()

    @pl.when(z == 2)
    def _():
        single(5, b1_slot(x, yh, 0), to_col(1, yl)).wait_recv()
        single(6, b1_slot(x, yh, 1), to_col(3, yl)).wait_recv()

    b_stream.send_own()
    swap(8, 0, own_piece)

    r_stream.send_pair()
    r_stream.relay_own()
    b_stream.send_pair()
    b_stream.relay_own()
    l_stream.send_pair()
    l_stream.relay_own()

    def swap_near(base, stream, slot):
        for number, (du, dv) in ((1, (0, 1)), (2, (-1, 0)), (3, (1, 0))):
            swap(base, number, slot(*stream._at(du, dv), None))

    swap_near(8, b_stream, b1_slot)
    swap_near(0, l_stream, left_slot)
    r_stream.relay_pair()
    b_stream.relay_pair()
    l_stream.relay_pair()
    for base, stream, slot in ((8, b_stream, b1_slot), (0, l_stream, left_slot)):
        for number, (du, dv) in ((4, (-1, 1)), (5, (1, 1))):
            swap(base, number, slot(*stream._at(du, dv), None))

    r_stream.end_own()
    b_stream.end_own()
    swap(8, 6, b1_slot(*b_stream._at(2, 0), None))
    l_stream.end_own()
    swap(0, 6, left_slot(*l_stream._at(2, 0), None))
    r_stream.end_pair()
    b_stream.end_pair()
    swap(8, 7, b1_slot(*b_stream._at(2, 1), None))
    l_stream.end_pair()
    swap(0, 7, left_slot(*l_stream._at(2, 1), None))

    order = ((0, 0), (0, 1), (-1, 0), (1, 0), (-1, 1), (1, 1), (2, 0), (2, 1))
    for number, (du, dv) in enumerate(order):
        for base, stream in ((8, b_stream), (0, l_stream)):
            uu, vv = stream._at(du, dv)
            if base == 8:
                theirs = b1t.at[2 * uu + vv, part((1 - core) * piece, piece, None), :]
            else:
                theirs = left.at[4 * vv + uu, part((1 - core) * width, width, None), :]
            pltpu.make_async_remote_copy(
                src_ref=theirs, dst_ref=theirs,
                send_sem=swap_send.at[base + number], recv_sem=swap_recv.at[base + number],
                device_id=other, device_id_type=MESH,
            ).wait_recv()

    rows = 512

    def products(k, first):
        def put(ref, tile, value):
            at = pl.ds(pl.multiple_of(tile * rows, rows), rows)
            if first:
                ref[at, :] = value
            else:
                ref[at, :] += value

        def over_left(tile, carry):
            lhs = left[k, pl.ds(pl.multiple_of(tile * rows, rows), rows), :]
            put(c_ref, tile, nn(lhs, right[k]))
            put(sr_ref, tile, nt(lhs, b1t[k]))
            return carry

        lax.fori_loop(0, height // rows, over_left, 0)

        def over_span(tile, carry):
            lhs = b1t[k, pl.ds(pl.multiple_of(tile * rows, rows), rows), :]
            put(sq_ref, tile, nn(lhs, right[k]))
            put(a_ref, tile, nt(lhs, b1t[k]))
            return carry

        lax.fori_loop(0, SPAN // rows, over_span, 0)

    products(0, True)

    def step(k, carry):
        products(k, False)
        return carry

    lax.fori_loop(1, 8, step, 0)

    for stream in (r_stream, b_stream, l_stream):
        stream.drain()
    for copy in swaps:
        copy.wait_send()

    @pl.when(jnp.logical_and(seed, core == 0))
    def _():
        single(1, mt_ref.at[pl.ds(piece, width - piece), :], other, spare).wait_send()

    @pl.when(seed)
    def _():
        single(2, own_piece, to_col(0, 1)).wait_send()

    @pl.when(z == 0)
    def _():
        single(3, own_piece, to_col(1, yl)).wait_send()
        single(4, own_piece, to_col(3, yl)).wait_send()

    @pl.when(z == 1)
    def _():
        single(5, b1_slot(x, yh, 0), to_col(2, yl)).wait_send()

    @pl.when(z == 3)
    def _():
        single(6, b1_slot(x, yh, 1), to_col(2, yl)).wait_send()


def gather_products(masked, transposed):
    depth, width = masked.shape
    height = 2 * width
    f32, bf16 = jnp.float32, jnp.bfloat16
    dma = pltpu.SemaphoreType.DMA
    hbm, vmem = pl.BlockSpec(memory_space=pl.ANY), pl.BlockSpec(memory_space=pltpu.VMEM)
    return pl.pallas_call(
        gather_kernel,
        out_shape=[
            jax.ShapeDtypeStruct((height, width), f32),
            jax.ShapeDtypeStruct((SPAN, SPAN), f32),
            jax.ShapeDtypeStruct((SPAN, width), f32),
            jax.ShapeDtypeStruct((height, SPAN), f32),
        ],
        in_specs=[hbm, hbm],
        out_specs=[vmem] * 4,
        scratch_shapes=[
            pltpu.VMEM((8, height, depth), bf16),
            pltpu.VMEM((8, depth, width), bf16),
            pltpu.VMEM((8, SPAN, depth), bf16),
            dma((3, 9)), dma((3, 9)),
            dma((16,)), dma((16,)),
            dma((7,)), dma((7,)),
            dma((3,)),
        ],
        compiler_params=pltpu.CompilerParams(
            collective_id=0, has_side_effects=True, vmem_limit_bytes=VMEM_LIMIT
        ),
        name="gather_products",
    )(masked, transposed)


def bc_row(x, k):
    return jnp.broadcast_to(x[k : k + 1, :], (8, NB))


def bc_col(x, j):
    return jnp.broadcast_to(x[:, j : j + 1], (8, NB))


def inverse_factor(block):
    groups = NB // 8
    lane = lax.broadcasted_iota(jnp.int32, (8, NB), 1)
    sub = lax.broadcasted_iota(jnp.int32, (8, NB), 0)
    s = [block[8 * g : 8 * g + 8, :] for g in range(groups)]
    y = [jnp.where(lane == sub + 8 * g, 1.0, 0.0) for g in range(groups)]
    out = []
    for g0 in range(groups):
        top, inv = s[g0], y[g0]
        pivots = [bc_col(top, 8 * g0 + k) for k in range(8)]
        below = {g: [bc_col(s[g], 8 * g0 + k) for k in range(8)] for g in range(g0 + 1, groups)}
        scale = jnp.zeros((8, NB), jnp.float32)
        done = jnp.zeros((8, NB), jnp.float32)
        for k in range(8):
            pivot = bc_row(pivots[k], k)
            reciprocal = 1.0 / pivot
            here = sub == k
            f = jnp.where(here, 0.0, pivots[k] * reciprocal)
            scale = jnp.where(here, reciprocal, scale)
            done = jnp.where(here, inv * lax.rsqrt(pivot), done)
            for m in range(k + 1, 8):
                pivots[m] = pivots[m] - f * bc_row(pivots[m], k)
            top = top - f * bc_row(top, k)
            inv = inv - f * bc_row(inv, k)
        out.append(done)
        if g0 + 1 < groups:
            top, inv = top * scale, inv * scale
            tops = [bc_row(top, k) for k in range(8)]
            invs = [bc_row(inv, k) for k in range(8)]
            for g in range(g0 + 1, groups):
                t = [below[g][k] * tops[k] for k in range(8)]
                v = [below[g][k] * invs[k] for k in range(8)]
                while len(t) > 1:
                    t = [t[i] + t[i + 1] for i in range(0, len(t), 2)]
                    v = [v[i] + v[i + 1] for i in range(0, len(v), 2)]
                s[g] = s[g] - t[0]
                y[g] = y[g] - v[0]
    return jnp.concatenate(out, axis=0)


def split(value):
    high = value.astype(jnp.bfloat16)
    return high, (value - high.astype(jnp.float32)).astype(jnp.bfloat16)


def finish_kernel(c_ref, a_in, sq_ref, sr_ref, out_ref, a_ref, y_ref, w_ref, xh_ref, xl_ref):
    row, col = lax.axis_index("row"), lax.axis_index("col")
    height, width = out_ref.shape
    blk = [slice(b * NB, (b + 1) * NB) for b in range(BLOCKS)]
    eye = jnp.where(
        lax.broadcasted_iota(jnp.int32, (NB, NB), 0) == lax.broadcasted_iota(jnp.int32, (NB, NB), 1),
        1.0, 0.0,
    )
    a_ref[...] = a_in[...]
    for b in range(BLOCKS):
        a_ref[blk[b], blk[b]] += eye
    w_ref[...] = sq_ref[...]
    for b in range(BLOCKS):
        y_ref[b] = inverse_factor(a_ref[blk[b], blk[b]])
        w_ref[blk[b], :] = nn_hi(y_ref[b], w_ref[blk[b], :])
        for i in range(b + 1, BLOCKS):
            a_ref[blk[i], blk[b]] = nt_hi(a_ref[blk[i], blk[b]], y_ref[b])
        for i in range(b + 1, BLOCKS):
            at = slice((b + 1) * NB, (i + 1) * NB)
            a_ref[blk[i], at] -= nt_hi(a_ref[blk[i], blk[b]], a_ref[at, blk[b]])
            w_ref[blk[i], :] -= nn_hi(a_ref[blk[i], blk[b]], w_ref[blk[b], :])

    cols = col * width + lax.broadcasted_iota(jnp.int32, (NB, width), 1)
    for b in range(BLOCKS):
        unit = jnp.where(b * NB + lax.broadcasted_iota(jnp.int32, (NB, width), 0) == cols, 1.0, 0.0)
        w_ref[blk[b], :] = jnp.where(cols < SPAN, unit, w_ref[blk[b], :])
    for b in reversed(range(BLOCKS)):
        solved = tn_hi(y_ref[b], w_ref[blk[b], :])
        xh_ref[blk[b], :], xl_ref[blk[b], :] = split(solved)
        for i in range(b):
            w_ref[blk[i], :] -= tn_hi(a_ref[blk[b], blk[i]], solved)

    rows = 256

    def tile(t, carry):
        at = pl.ds(pl.multiple_of(t * rows, rows), rows)
        first = row * height + t * rows
        grow = first + lax.broadcasted_iota(jnp.int32, (rows, width), 0)
        gcol = col * width + lax.broadcasted_iota(jnp.int32, (rows, width), 1)
        srow = first + lax.broadcasted_iota(jnp.int32, (rows, SPAN), 0)
        scol = lax.broadcasted_iota(jnp.int32, (rows, SPAN), 1)
        sh, sl = split(sr_ref[at, :] + jnp.where(srow == scol, 1.0, 0.0))
        value = nn(sh, xh_ref[...]) + nn(sl, xh_ref[...]) + nn(sh, xl_ref[...])
        system = c_ref[at, :] + jnp.where(grow == gcol, 1.0, 0.0)
        lead = jnp.where(grow >= gcol, value, 0.0)
        rest = jnp.where(grow < SPAN, 0.0, system - value)
        out_ref[at, :] = jnp.where(gcol < SPAN, lead, rest)
        return carry

    lax.fori_loop(0, height // rows, tile, 0)


def finish(c, a, sq, sr):
    height, width = c.shape
    f32, bf16 = jnp.float32, jnp.bfloat16
    vmem = pl.BlockSpec(memory_space=pltpu.VMEM)
    return pl.pallas_call(
        finish_kernel,
        out_shape=jax.ShapeDtypeStruct((height, width), f32),
        in_specs=[vmem] * 4,
        out_specs=vmem,
        scratch_shapes=[
            pltpu.VMEM((SPAN, SPAN), f32),
            pltpu.VMEM((BLOCKS, NB, NB), f32),
            pltpu.VMEM((SPAN, width), f32),
            pltpu.VMEM((SPAN, width), bf16),
            pltpu.VMEM((SPAN, width), bf16),
        ],
        compiler_params=pltpu.CompilerParams(vmem_limit_bytes=VMEM_LIMIT),
        name="finish",
    )(c, a, sq, sr)


def expand_tiles(blocks):
    return jnp.repeat(jnp.repeat(blocks, TILE, axis=0), TILE, axis=1)


def on_device(b_values, tile_mask):
    row_index = lax.axis_index("row")
    col_index = lax.axis_index("col")
    depth, width = b_values.shape
    occupancy = lax.dynamic_slice(
        tile_mask,
        (row_index * (depth // TILE), col_index * (width // TILE)),
        (depth // TILE, width // TILE),
    )
    masked = b_values * expand_tiles(occupancy).astype(jnp.bfloat16)
    return finish(*gather_products(masked, masked.T))


def solution(mesh):
    return jax.shard_map(
        on_device,
        mesh=mesh,
        in_specs=(P("row", "col"), P()),
        out_specs=P("row", "col"),
        check_vma=False,
    )
```

time: 998 us -> 299 us (0.30)
  the two profiles are of different devices: /device:TPU:0 before, /device:TPU:89 now
where the time goes in v1:
time: 299 us; the launch traced here: 295 us
  Pallas kernels  291 us (97%)
    pallas_call x1, Pallas kernels, gather_products(): pl.pallas_call(gather_kernel, out_shape=[jax.ShapeDtypeStruct((height, wi...  213 us
    pallas_call x1, Pallas kernels, finish(): pl.pallas_call(finish_kernel, out_shape=jax.ShapeDtypeStruct((height, wid...  77.5 us

profile of v1, /device:TPU:89, one launch (start us, length us, event | category | flops | bytes accessed | tf_op | source)
XLA Modules:
  0.0 294.7 jit_solution(3885882756946766512)
XLA Ops:
  0.0 0.8 dynamic-slice_convert_fusion
  0.8 0.1 copy.3
  0.9 0.1 broadcast_bitcast_fusion
  1.0 1.4 copy.4
  2.4 0.1 bitcast_multiply_fusion
  2.4 0.0 copy-start
  2.4 1.2 copy.5.m_ref
  3.6 0.0 copy-done
  3.6 213.4 %gather_products.1 = (f32[1536,768]{1,0:T(8,128)}, f32[1024,1024]{1,0:T(8,128)}, f32[1024,768]{1,0:T(8,128)}, f32[1536,1024]{1,0:T(8,128)}) custom-call(bf16[512,768]{1,0:T(8,128)(2,1)} %copy.5.m_ref, bf16[768,512]{1,0:T(8,128)(2,1)} %bitcast.8), custom_call_target="tpu_custom_call" | custom-call | tf_op jit(solution)/shard_map/gather_products/pallas_call | solution.py:374
  217.1 77.5 %finish.1 = f32[1536,768]{1,0:T(8,128)} custom-call(f32[1536,768]{1,0:T(8,128)} %get-tuple-element.9.c_ref, f32[1024,1024]{1,0:T(8,128)} %get-tuple-element.10.a_in, f32[1024,768]{1,0:T(8,128)} %get-tuple-element.11.sq_ref, f32[1536,1024]{1,0:T(8,128)} %get-tuple-element.12.sr_ref), custom_call_target="tpu_custom_call" | custom-call | tf_op jit(solution)/shard_map/finish/pallas_call | solution.py:509
  (1 shorter events, 0.0 us)
Async XLA Ops:
  2.4 1.2 copy-start

commit v2 on v0

v2 whole, which is shorter than its diff:
```python
import functools

import jax
import jax.numpy as jnp
from jax import lax
from jax.experimental import pallas as pl
from jax.experimental.pallas import tpu as pltpu
from jax.sharding import PartitionSpec as P

TILE = 256
PANEL = 512
SPAN = 2 * PANEL
NB = 128
BLOCKS = SPAN // NB
MESH = pl.DeviceIdType.MESH
VMEM_LIMIT = 66_000_000


def nn(a, b):
    return lax.dot_general(a, b, (((1,), (0,)), ((), ())), preferred_element_type=jnp.float32)


def nt(a, b):
    return lax.dot_general(a, b, (((1,), (1,)), ((), ())), preferred_element_type=jnp.float32)


def tn(a, b):
    return lax.dot_general(a, b, (((0,), (0,)), ((), ())), preferred_element_type=jnp.float32)


def split(value):
    high = value.astype(jnp.bfloat16)
    return high, (value - high.astype(jnp.float32)).astype(jnp.bfloat16)


def three(dot, a, b):
    (ah, al), (bh, bl) = a, b
    return dot(ah, bh) + (dot(al, bh) + dot(ah, bl))


class Stream:
    def __init__(self, index, send, recv, slot, device, u, v):
        self.index, self.send, self.recv = index, send, recv
        self.slot, self.device, self.u, self.v = slot, device, u, v
        self.sent = []
        self.ring = {du: lax.rem(u + du + 4, 4) for du in (-1, 0, 1, 2)}
        self.pair = {0: v, 1: 1 - v}
        self.zero = 0

    def _at(self, du, dv):
        return self.ring[du], self.pair[dv]

    def _copy(self, label, ref, du, dv):
        uu, vv = self._at(du, dv)
        return pltpu.make_async_remote_copy(
            src_ref=ref,
            dst_ref=ref,
            send_sem=self.send.at[self.index + self.zero, label + self.zero],
            recv_sem=self.recv.at[self.index + self.zero, label + self.zero],
            device_id=self.device(uu, vv),
            device_id_type=MESH,
        )

    def push(self, label, block, half, to):
        copy = self._copy(label, self.slot(*self._at(*block), half), *to)
        copy.start()
        self.sent.append((label, block, half, to))

    def arrived(self, label, block, half, source):
        self._copy(label, self.slot(*self._at(*block), half), *source).wait_recv()

    def send_own(self):
        self.push(0, (0, 0), None, (0, 1))
        self.push(1, (0, 0), None, (1, 0))
        self.push(2, (0, 0), None, (-1, 0))

    def send_pair(self):
        self.arrived(0, (0, 1), None, (0, 1))
        self.push(3, (0, 1), None, (1, 0))
        self.push(4, (0, 1), None, (-1, 0))

    def relay_own(self):
        self.arrived(1, (-1, 0), None, (-1, 0))
        self.push(5, (-1, 0), 0, (1, 0))
        self.arrived(2, (1, 0), None, (1, 0))
        self.push(6, (1, 0), 1, (-1, 0))

    def relay_pair(self):
        self.arrived(3, (-1, 1), None, (-1, 0))
        self.push(7, (-1, 1), 0, (1, 0))
        self.arrived(4, (1, 1), None, (1, 0))
        self.push(8, (1, 1), 1, (-1, 0))

    def end_own(self):
        self.arrived(5, (2, 0), 0, (-1, 0))
        self.arrived(6, (2, 0), 1, (1, 0))

    def end_pair(self):
        self.arrived(7, (2, 1), 0, (-1, 0))
        self.arrived(8, (2, 1), 1, (1, 0))

    def drain(self):
        for label, block, half, to in self.sent:
            self._copy(label, self.slot(*self._at(*block), half), *to).wait_send()


def bc_row(x, k):
    return jnp.broadcast_to(x[k : k + 1, :], (8, NB))


def bc_col(x, j):
    return jnp.broadcast_to(x[:, j : j + 1], (8, NB))


def inverse_factor(block):
    groups = NB // 8
    lane = lax.broadcasted_iota(jnp.int32, (8, NB), 1)
    sub = lax.broadcasted_iota(jnp.int32, (8, NB), 0)
    s = [block[8 * g : 8 * g + 8, :] for g in range(groups)]
    y = [jnp.where(lane == sub + 8 * g, 1.0, 0.0) for g in range(groups)]
    out = []
    for g0 in range(groups):
        top, inv = s[g0], y[g0]
        pivots = [bc_col(top, 8 * g0 + k) for k in range(8)]
        below = {g: [bc_col(s[g], 8 * g0 + k) for k in range(8)] for g in range(g0 + 1, groups)}
        scale = jnp.zeros((8, NB), jnp.float32)
        done = jnp.zeros((8, NB), jnp.float32)
        for k in range(8):
            pivot = bc_row(pivots[k], k)
            reciprocal = 1.0 / pivot
            here = sub == k
            f = jnp.where(here, 0.0, pivots[k] * reciprocal)
            scale = jnp.where(here, reciprocal, scale)
            done = jnp.where(here, inv * lax.rsqrt(pivot), done)
            for m in range(k + 1, 8):
                pivots[m] = pivots[m] - f * bc_row(pivots[m], k)
            top = top - f * bc_row(top, k)
            inv = inv - f * bc_row(inv, k)
        out.append(done)
        if g0 + 1 < groups:
            top, inv = top * scale, inv * scale
            tops = [bc_row(top, k) for k in range(8)]
            invs = [bc_row(inv, k) for k in range(8)]
            for g in range(g0 + 1, groups):
                t = [below[g][k] * tops[k] for k in range(8)]
                v = [below[g][k] * invs[k] for k in range(8)]
                while len(t) > 1:
                    t = [t[i] + t[i + 1] for i in range(0, len(t), 2)]
                    v = [v[i] + v[i + 1] for i in range(0, len(v), 2)]
                s[g] = s[g] - t[0]
                y[g] = y[g] - v[0]
    return jnp.concatenate(out, axis=0)


def whole_kernel(
    m_ref, mt_ref, out_ref,
    left, right, b1t, a_ref, sq_ref, sr_ref, linv_ref, xh_ref, xl_ref,
    send, recv, swap_send, swap_recv, one_send, one_recv, local,
):
    row, col = lax.axis_index("row"), lax.axis_index("col")
    x, yh = lax.div(row, 2), lax.rem(row, 2)
    core, q = lax.rem(col, 2), lax.div(col, 2)
    yl, z = lax.div(q, 4), lax.rem(q, 4)
    depth, width = m_ref.shape
    height = 2 * width
    piece = SPAN // 2
    other = (row, q * 2 + 1 - core)

    def over_row(u, v):
        return (2 * u + v, col)

    def over_col(u, v):
        return (row, (4 * v + u) * 2 + core)

    def part(start, size, half):
        if half is None:
            return pl.ds(pl.multiple_of(start, 128), size)
        return pl.ds(pl.multiple_of(start + half * (size // 2), 128), size // 2)

    def right_slot(u, v, half):
        return right.at[2 * u + v, part(0, depth, half), :]

    def left_slot(u, v, half, side=core):
        return left.at[4 * v + u, part(side * width, width, half), :]

    def b1_slot(u, v, half, side=core):
        return b1t.at[2 * u + v, part(side * piece, piece, half), :]

    r_stream = Stream(0, send, recv, right_slot, over_row, x, yh)
    b_stream = Stream(1, send, recv, b1_slot, over_row, x, yh)
    l_stream = Stream(2, send, recv, left_slot, over_col, z, yl)
    order = ((0, 0), (0, 1), (-1, 0), (1, 0), (-1, 1), (1, 1), (2, 0), (2, 1))
    swaps = []

    def swap_copy(base, number, ref):
        place = base + number + l_stream.zero
        return pltpu.make_async_remote_copy(
            src_ref=ref, dst_ref=ref,
            send_sem=swap_send.at[place], recv_sem=swap_recv.at[place],
            device_id=other, device_id_type=MESH,
        )

    def swap_out(base, number):
        stream, slot = (b_stream, b1_slot) if base == 8 else (l_stream, left_slot)
        return swap_copy(base, number, slot(*stream._at(*order[number]), None))

    def swap(base, number):
        swap_out(base, number).start()
        swaps.append((base, number))

    def swapped(base, number):
        stream, slot = (b_stream, b1_slot) if base == 8 else (l_stream, left_slot)
        theirs = slot(*stream._at(*order[number]), None, 1 - core)
        swap_copy(base, number, theirs).wait_recv()

    def single(number, ref, target, place=None):
        return pltpu.make_async_remote_copy(
            src_ref=ref, dst_ref=ref if place is None else place,
            send_sem=one_send.at[number], recv_sem=one_recv.at[number],
            device_id=target, device_id_type=MESH,
        )

    own_right = pltpu.make_async_copy(m_ref, right.at[row], local.at[0])
    own_right.start()

    barrier = pltpu.get_barrier_semaphore()
    mirror = (q, 2 * row + core)
    friends = [
        over_row(lax.rem(x + 1, 4), yh), over_row(lax.rem(x + 3, 4), yh), over_row(x, 1 - yh),
        over_col(lax.rem(z + 1, 4), yl), over_col(lax.rem(z + 3, 4), yl), over_col(z, 1 - yl),
        other,
    ]
    for friend in friends:
        pl.semaphore_signal(barrier, inc=1, device_id=friend, device_id_type=MESH)

    @pl.when(row != q)
    def _():
        pl.semaphore_signal(barrier, inc=1, device_id=mirror, device_id_type=MESH)
        pl.semaphore_wait(barrier, len(friends) + 1)

    @pl.when(row == q)
    def _():
        pl.semaphore_wait(barrier, len(friends))

    seed = jnp.logical_and(yl == 0, z == 0)
    spare = b1t.at[row, pl.ds(piece, width - piece), :]
    low = b1t.at[row, pl.ds(0, piece), :]
    high = b1t.at[row, pl.ds(width, SPAN - width), :]
    chunk = [b1_slot(x, yh, 0), b1_slot(x, yh, 1)]

    @pl.when(jnp.logical_and(seed, core == 0))
    def _():
        single(1, mt_ref.at[pl.ds(piece, width - piece), :], other, spare).start()
        copy = pltpu.make_async_copy(mt_ref.at[pl.ds(0, piece), :], low, local.at[2])
        copy.start()
        copy.wait()

    @pl.when(jnp.logical_and(seed, core == 1))
    def _():
        copy = pltpu.make_async_copy(mt_ref.at[pl.ds(0, SPAN - width), :], high, local.at[2])
        copy.start()
        copy.wait()
        single(1, spare, other).wait_recv()

    def down(h):
        single(4 + h, chunk[h], over_col(1, yl)).start()

    def up(h):
        single(6 + h, chunk[h], over_col(3, yl)).start()

    @pl.when(seed)
    def _():
        for h in range(2):
            single(2 + h, chunk[h], over_col(0, 1)).start()
            down(h)
            up(1 - h)

    mine = part(core * width, width, None)

    @pl.when(row != q)
    def _():
        single(0, mt_ref, mirror, left.at[row, mine, :]).start()

    @pl.when(row == q)
    def _():
        pltpu.make_async_copy(mt_ref, left.at[row, mine, :], local.at[1]).start()

    own_right.wait()
    r_stream.push(1, (0, 0), None, (1, 0))
    r_stream.push(2, (0, 0), None, (-1, 0))

    @pl.when(jnp.logical_and(z == 0, yl == 1))
    def _():
        for h in range(2):
            single(2 + h, chunk[h], over_col(0, 0)).wait_recv()
            down(h)
            up(h)

    @pl.when(z == 1)
    def _():
        single(4, chunk[0], over_col(0, yl)).wait_recv()
        single(8, chunk[0], over_col(2, yl)).start()
        single(5, chunk[1], over_col(0, yl)).wait_recv()

    @pl.when(z == 3)
    def _():
        single(7, chunk[1], over_col(0, yl)).wait_recv()
        single(9, chunk[1], over_col(2, yl)).start()
        single(6, chunk[0], over_col(0, yl)).wait_recv()

    @pl.when(z == 2)
    def _():
        single(8, chunk[0], over_col(1, yl)).wait_recv()
        single(9, chunk[1], over_col(3, yl)).wait_recv()

    b_stream.send_own()
    swap(8, 0)
    r_stream.push(0, (0, 0), None, (0, 1))

    rows = 512

    def at_tile(tile):
        return pl.ds(pl.multiple_of(tile * rows, rows), rows)

    def gram(number):
        swapped(8, number)
        uu, vv = b_stream._at(*order[number])
        k = 2 * uu + vv

        def over_span(tile, carry):
            value = nt(b1t[k, at_tile(tile), :], b1t[k])
            if number == 0:
                a_ref[at_tile(tile), :] = value
            else:
                a_ref[at_tile(tile), :] += value
            return carry

        lax.fori_loop(0, SPAN // rows, over_span, 0)

    b_stream.send_pair()
    swap(8, 1)
    gram(0)
    b_stream.relay_own()
    swap(8, 2)
    swap(8, 3)
    gram(1)
    b_stream.relay_pair()
    swap(8, 4)
    swap(8, 5)
    r_stream.send_pair()
    r_stream.relay_own()
    gram(2)
    gram(3)
    b_stream.end_own()
    swap(8, 6)
    gram(4)
    gram(5)

    @pl.when(row != q)
    def _():
        single(0, mt_ref, mirror, left.at[q, mine, :]).wait()

    @pl.when(row == q)
    def _():
        pltpu.make_async_copy(mt_ref, left.at[row, mine, :], local.at[1]).wait()

    l_stream.send_own()
    swap(0, 0)
    b_stream.end_pair()
    swap(8, 7)
    gram(6)
    gram(7)

    eye = jnp.where(
        lax.broadcasted_iota(jnp.int32, (NB, NB), 0) == lax.broadcasted_iota(jnp.int32, (NB, NB), 1),
        1.0, 0.0,
    )
    for b in range(BLOCKS):
        at = slice(b * NB, (b + 1) * NB)
        a_ref[at, at] += eye
    linv_ref[...] = jnp.zeros_like(linv_ref)
    tall = 256

    def factor_step(b, carry):
        r_stream.zero = l_stream.zero = b * 0
        at = pl.ds(pl.multiple_of(b * NB, NB), NB)
        y = inverse_factor(a_ref[at, at])
        linv_ref[at, at] = y
        below = lax.broadcasted_iota(jnp.int32, (SPAN, NB), 0) >= (b + 1) * NB
        panel = three(nt, split(a_ref[:, at]), split(y))
        panel = jnp.where(below, panel, 0.0)
        a_ref[:, at] = panel
        xh_ref[:, 0:NB], xl_ref[:, 0:NB] = split(panel)

        def update(tile, c):
            part_rows = pl.ds(pl.multiple_of(tile * tall, tall), tall)
            a_ref[part_rows, :] -= three(
                nt,
                (xh_ref[part_rows, 0:NB], xl_ref[part_rows, 0:NB]),
                (xh_ref[:, 0:NB], xl_ref[:, 0:NB]),
            )
            return c

        lax.fori_loop((b + 1) // 2, SPAN // tall, update, 0)

        @pl.when(b == 1)
        def _():
            r_stream.relay_pair()

        @pl.when(b == 2)
        def _():
            l_stream.send_pair()
            swap(0, 1)
            l_stream.relay_own()
            swap(0, 2)
            swap(0, 3)

        @pl.when(b == 5)
        def _():
            l_stream.relay_pair()
            swap(0, 4)
            swap(0, 5)

        return carry

    lax.fori_loop(0, BLOCKS, factor_step, 0)
    r_stream.zero = l_stream.zero = 0

    r_stream.end_own()
    r_stream.end_pair()

    def over_blocks(ref, tiles, rhs):
        def step(k, carry):
            def inner(tile, c):
                value = rhs(k, at_tile(tile))

                @pl.when(k == 0)
                def _():
                    ref[at_tile(tile), :] = value

                @pl.when(k > 0)
                def _():
                    ref[at_tile(tile), :] += value

                return c

            return lax.fori_loop(0, tiles, inner, carry)

        lax.fori_loop(0, 8, step, 0)

    over_blocks(sq_ref, SPAN // rows, lambda k, at: nn(b1t[k, at, :], right[k]))
    l_stream.end_own()
    swap(0, 6)
    l_stream.end_pair()
    swap(0, 7)

    size = NB
    while size < SPAN:
        for lo in range(0, SPAN, 2 * size):
            one, two = slice(lo, lo + size), slice(lo + size, lo + 2 * size)
            inner = three(nn, split(a_ref[two, one]), split(linv_ref[one, one]))
            linv_ref[two, one] = -three(nn, split(linv_ref[two, two]), split(inner))
        size *= 2

    cols = col * width + lax.broadcasted_iota(jnp.int32, (tall, width), 1)
    for b in range(SPAN // tall):
        at = slice(b * tall, (b + 1) * tall)
        upto = slice(0, (b + 1) * tall)
        solved = three(nn, split(linv_ref[at, upto]), split(sq_ref[upto, :]))
        unit = jnp.where(b * tall + lax.broadcasted_iota(jnp.int32, (tall, width), 0) == cols, 1.0, 0.0)
        xh_ref[at, :], xl_ref[at, :] = split(jnp.where(cols < SPAN, unit, solved))
    for b in range(SPAN // tall):
        at = slice(b * tall, (b + 1) * tall)
        onward = slice(b * tall, SPAN)
        sq_ref[at, :] = three(tn, split(linv_ref[onward, at]), (xh_ref[onward, :], xl_ref[onward, :]))
    for b in range(SPAN // tall):
        at = slice(b * tall, (b + 1) * tall)
        xh_ref[at, :], xl_ref[at, :] = split(sq_ref[at, :])

    for number in range(8):
        swapped(0, number)
    over_blocks(out_ref, height // rows, lambda k, at: nn(left[k, at, :], right[k]))
    over_blocks(sr_ref, height // rows, lambda k, at: nt(left[k, at, :], b1t[k]))

    def finish(t, carry):
        at = pl.ds(pl.multiple_of(t * tall, tall), tall)
        first = row * height + t * tall
        grow = first + lax.broadcasted_iota(jnp.int32, (tall, width), 0)
        gcol = col * width + lax.broadcasted_iota(jnp.int32, (tall, width), 1)
        srow = first + lax.broadcasted_iota(jnp.int32, (tall, SPAN), 0)
        scol = lax.broadcasted_iota(jnp.int32, (tall, SPAN), 1)
        strip = split(sr_ref[at, :] + jnp.where(srow == scol, 1.0, 0.0))
        value = three(nn, strip, (xh_ref[...], xl_ref[...]))
        system = out_ref[at, :] + jnp.where(grow == gcol, 1.0, 0.0)
        lead = jnp.where(grow >= gcol, value, 0.0)
        rest = jnp.where(grow < SPAN, 0.0, system - value)
        out_ref[at, :] = jnp.where(gcol < SPAN, lead, rest)
        return carry

    lax.fori_loop(0, height // tall, finish, 0)

    for stream in (r_stream, b_stream, l_stream):
        stream.drain()
    for base, number in swaps:
        swap_out(base, number).wait_send()

    @pl.when(jnp.logical_and(seed, core == 0))
    def _():
        single(1, mt_ref.at[pl.ds(piece, width - piece), :], other, spare).wait_send()

    @pl.when(seed)
    def _():
        for h in range(2):
            single(2 + h, chunk[h], over_col(0, 1)).wait_send()

    @pl.when(z == 0)
    def _():
        for h in range(2):
            single(4 + h, chunk[h], over_col(1, yl)).wait_send()
            single(6 + h, chunk[h], over_col(3, yl)).wait_send()

    @pl.when(z == 1)
    def _():
        single(8, chunk[0], over_col(2, yl)).wait_send()

    @pl.when(z == 3)
    def _():
        single(9, chunk[1], over_col(2, yl)).wait_send()


def whole(masked, transposed):
    depth, width = masked.shape
    height = 2 * width
    f32, bf16 = jnp.float32, jnp.bfloat16
    dma = pltpu.SemaphoreType.DMA
    hbm, vmem = pl.BlockSpec(memory_space=pl.ANY), pl.BlockSpec(memory_space=pltpu.VMEM)
    return pl.pallas_call(
        whole_kernel,
        out_shape=jax.ShapeDtypeStruct((height, width), f32),
        in_specs=[hbm, hbm],
        out_specs=vmem,
        scratch_shapes=[
            pltpu.VMEM((8, height, depth), bf16),
            pltpu.VMEM((8, depth, width), bf16),
            pltpu.VMEM((8, SPAN, depth), bf16),
            pltpu.VMEM((SPAN, SPAN), f32),
            pltpu.VMEM((SPAN, width), f32),
            pltpu.VMEM((height, SPAN), f32),
            pltpu.VMEM((SPAN, SPAN), f32),
            pltpu.VMEM((SPAN, width), bf16),
            pltpu.VMEM((SPAN, width), bf16),
            dma((3, 9)), dma((3, 9)),
            dma((16,)), dma((16,)),
            dma((10,)), dma((10,)),
            dma((3,)),
        ],
        compiler_params=pltpu.CompilerParams(
            collective_id=0, has_side_effects=True, vmem_limit_bytes=VMEM_LIMIT
        ),
        name="whole",
    )(masked, transposed)


def expand_tiles(blocks):
    return jnp.repeat(jnp.repeat(blocks, TILE, axis=0), TILE, axis=1)


def on_device(b_values, tile_mask):
    row_index = lax.axis_index("row")
    col_index = lax.axis_index("col")
    depth, width = b_values.shape
    occupancy = lax.dynamic_slice(
        tile_mask,
        (row_index * (depth // TILE), col_index * (width // TILE)),
        (depth // TILE, width // TILE),
    )
    masked = b_values * expand_tiles(occupancy).astype(jnp.bfloat16)
    return whole(masked, masked.T)


def solution(mesh):
    return jax.shard_map(
        on_device,
        mesh=mesh,
        in_specs=(P("row", "col"), P()),
        out_specs=P("row", "col"),
        check_vma=False,
    )
```

time: 998 us -> 242 us (0.24)
  waiting for transfers between devices: 519 us -> 0 us
  other arithmetic: 271 us -> 0.82 us
  Pallas kernels: 0 us -> 229 us
  matrix products: 113 us -> 0 us
  local copies, waits for them, and re-layouts: 65.9 us -> 7.59 us
  between operations: 20.2 us -> 0.03 us
    psum x2 -> x0, waiting for transfers between devices: 294 us -> none  [spread(): return lax.psum(block, axis)]
    another operation x34 -> x0, other arithmetic: 248 us -> none  [the longest x29 166 us: factor_top(): jnp.linalg.cholesky(updated[lower_edge:upper_edge, lower_edge:upper_edge])]
    pallas_call x0 -> x1, Pallas kernels: none -> 229 us  [whole(): pl.pallas_call(whole_kernel, out_shape=jax.ShapeDtypeStruct((height, widt...]
    all_gather x3 -> x0, waiting for transfers between devices: 148 us -> none  [the longest x1 101 us: on_device(): columns = lax.all_gather(masked, 'row', axis=0, tiled=True)]
    unnamed x7 -> x0, waiting for transfers between devices: 76.9 us -> none
    another operation x47 -> x0, matrix products: 61.4 us -> none  [the longest x28 48.5 us: panel_rows(): jax.scipy.linalg.solve_triangular(factor[lower_edge:upper_edge, lower_edg...]
    dot_general x5 -> x0, matrix products: 51.8 us -> none  [the longest x1 18.9 us: on_device(): lax.dot_general(left_factor, columns, (((0,), (0,)), ((), ())), preferred...]
    another operation x41 -> x0, local copies, waits for them, and re-layouts: 31.1 us -> none  [the longest x33 29.9 us: panel_rows(): jax.scipy.linalg.solve_triangular(factor[lower_edge:upper_edge, lower_edg...]
  transfers between devices with their start and end apart: 6 -> 0, of which waited for: 5 -> 0; matrix products, arithmetic and copies ran while one was open for 37% -> 0% of each run, Pallas kernels for 0% -> 0%
where the time goes in v2:
time: 242 us; the launch traced here: 238 us
  Pallas kernels  229 us (95%)
  local copies, waits for them, and re-layouts  7.59 us (3%)
    pallas_call x1, Pallas kernels, whole(): pl.pallas_call(whole_kernel, out_shape=jax.ShapeDtypeStruct((height, widt...  229 us
    unnamed x6, local copies, waits for them, and re-layouts  6.33 us

profile of v2, /device:TPU:0, one launch (start us, length us, event | category | flops | bytes accessed | tf_op | source)
XLA Modules:
  0.0 237.9 jit_solution(7826863697165010779)
XLA Ops:
  0.0 0.8 dynamic-slice_convert_fusion
  0.8 0.1 copy.3
  0.9 0.1 broadcast_bitcast_fusion
  1.0 1.4 copy.4
  2.4 0.1 bitcast_multiply_fusion
  2.4 0.0 copy-start
  2.4 1.2 copy.5.m_ref
  3.6 0.0 copy-done
  3.6 229.5 %whole.1 = f32[1536,768]{1,0:T(8,128)} custom-call(bf16[512,768]{1,0:T(8,128)(2,1)} %copy.5.m_ref, bf16[768,512]{1,0:T(8,128)(2,1)} %bitcast.8), custom_call_target="tpu_custom_call" | custom-call | tf_op jit(solution)/shard_map/whole/pallas_call | solution.py:537
  233.1 4.8 %copy.8 = f32[1536,768]{1,0:T(8,128)} copy(f32[1536,768]{1,0:T(8,128)} %whole.1) | data formatting | bytes 9437184
  (1 shorter events, 0.0 us)
Async XLA Ops:
  2.4 1.2 copy-start

commit v3 on v2

--- a/solution.py
+++ b/solution.py
@@ -154,7 +154,7 @@
 
 def whole_kernel(
     m_ref, mt_ref, out_ref,
-    left, right, b1t, a_ref, sq_ref, sr_ref, linv_ref, xh_ref, xl_ref,
+    left, right, b1t, stage, a_ref, sq_ref, sh_ref, sl_ref, linv_ref, xh_ref, xl_ref,
     send, recv, swap_send, swap_recv, one_send, one_recv, local,
 ):
     row, col = lax.axis_index("row"), lax.axis_index("col")
@@ -180,8 +180,20 @@
     def right_slot(u, v, half):
         return right.at[2 * u + v, part(0, depth, half), :]
 
+    def flip(a, b):
+        return a + b - 2 * a * b
+
+    r2, r1 = lax.div(x, 2), lax.rem(x, 2)
+
+    def crossed(u, v):
+        return 4 * flip(r2, v) + 2 * flip(r1, lax.div(u, 2)) + flip(yh, lax.rem(u, 2))
+
+    cross = crossed(z, yl)
+    blocks = {(du, dv): crossed(lax.rem(z + du + 4, 4), yl if dv == 0 else 1 - yl)
+              for du in (-1, 0, 1, 2) for dv in (0, 1)}
+
     def left_slot(u, v, half, side=core):
-        return left.at[4 * v + u, part(side * width, width, half), :]
+        return left.at[crossed(u, v), part(side * width, width, half), :]
 
     def b1_slot(u, v, half, side=core):
         return b1t.at[2 * u + v, part(side * piece, piece, half), :]
@@ -224,7 +236,7 @@
     own_right.start()
 
     barrier = pltpu.get_barrier_semaphore()
-    mirror = (q, 2 * row + core)
+    inside, across = (row, 2 * cross + core), (cross, col)
     friends = [
         over_row(lax.rem(x + 1, 4), yh), over_row(lax.rem(x + 3, 4), yh), over_row(x, 1 - yh),
         over_col(lax.rem(z + 1, 4), yl), over_col(lax.rem(z + 3, 4), yl), over_col(z, 1 - yl),
@@ -233,14 +245,21 @@
     for friend in friends:
         pl.semaphore_signal(barrier, inc=1, device_id=friend, device_id_type=MESH)
 
-    @pl.when(row != q)
-    def _():
-        pl.semaphore_signal(barrier, inc=1, device_id=mirror, device_id_type=MESH)
-        pl.semaphore_wait(barrier, len(friends) + 1)
-
-    @pl.when(row == q)
-    def _():
-        pl.semaphore_wait(barrier, len(friends))
+    moves_in, moves_across = row != 0, q != 0
+    for moves, friend in ((moves_in, inside), (moves_across, across)):
+        @pl.when(moves)
+        def _(friend=friend):
+            pl.semaphore_signal(barrier, inc=1, device_id=friend, device_id_type=MESH)
+
+    for one in (0, 1):
+        for two in (0, 1):
+            here = jnp.logical_and(
+                moves_in if one else row == 0, moves_across if two else q == 0
+            )
+
+            @pl.when(here)
+            def _(count=len(friends) + one + two):
+                pl.semaphore_wait(barrier, count)
 
     seed = jnp.logical_and(yl == 0, z == 0)
     spare = b1t.at[row, pl.ds(piece, width - piece), :]
@@ -275,15 +294,29 @@
             down(h)
             up(1 - h)
 
-    mine = part(core * width, width, None)
-
-    @pl.when(row != q)
-    def _():
-        single(0, mt_ref, mirror, left.at[row, mine, :]).start()
-
-    @pl.when(row == q)
-    def _():
-        pltpu.make_async_copy(mt_ref, left.at[row, mine, :], local.at[1]).start()
+    def mine(h):
+        return part(core * width, width, h)
+
+    def along(h):
+        at = part(0, width, h)
+        return single(10 + h, mt_ref.at[at, :], inside, stage.at[at, :])
+
+    def over(h, slot):
+        return single(12 + h, stage.at[part(0, width, h), :], across, left.at[slot, mine(h), :])
+
+    def still(h):
+        return pltpu.make_async_copy(
+            stage.at[part(0, width, h), :], left.at[cross, mine(h), :], local.at[3 + h]
+        )
+
+    @pl.when(moves_in)
+    def _():
+        along(0).start()
+        along(1).start()
+
+    @pl.when(row == 0)
+    def _():
+        pltpu.make_async_copy(mt_ref, stage, local.at[1]).start()
 
     own_right.wait()
     r_stream.push(1, (0, 0), None, (1, 0))
@@ -315,6 +348,24 @@
 
     b_stream.send_own()
     swap(8, 0)
+
+    @pl.when(row == 0)
+    def _():
+        pltpu.make_async_copy(mt_ref, stage, local.at[1]).wait()
+
+    for h in range(2):
+        @pl.when(moves_in)
+        def _(h=h):
+            along(h).wait_recv()
+
+        @pl.when(moves_across)
+        def _(h=h):
+            over(h, row).start()
+
+        @pl.when(q == 0)
+        def _(h=h):
+            still(h).start()
+
     r_stream.push(0, (0, 0), None, (0, 1))
 
     rows = 512
@@ -339,10 +390,22 @@
 
     b_stream.send_pair()
     swap(8, 1)
-    gram(0)
     b_stream.relay_own()
     swap(8, 2)
     swap(8, 3)
+
+    for h in range(2):
+        @pl.when(moves_across)
+        def _(h=h):
+            over(h, cross).wait_recv()
+
+        @pl.when(q == 0)
+        def _(h=h):
+            still(h).wait()
+
+    l_stream.send_own()
+    swap(0, 0)
+    gram(0)
     gram(1)
     b_stream.relay_pair()
     swap(8, 4)
@@ -351,21 +414,15 @@
     r_stream.relay_own()
     gram(2)
     gram(3)
+    l_stream.send_pair()
+    swap(0, 1)
+    l_stream.relay_own()
+    swap(0, 2)
+    swap(0, 3)
     b_stream.end_own()
     swap(8, 6)
     gram(4)
     gram(5)
-
-    @pl.when(row != q)
-    def _():
-        single(0, mt_ref, mirror, left.at[q, mine, :]).wait()
-
-    @pl.when(row == q)
-    def _():
-        pltpu.make_async_copy(mt_ref, left.at[row, mine, :], local.at[1]).wait()
-
-    l_stream.send_own()
-    swap(0, 0)
     b_stream.end_pair()
     swap(8, 7)
     gram(6)
@@ -381,11 +438,52 @@
     linv_ref[...] = jnp.zeros_like(linv_ref)
     tall = 256
 
+    right_order = [2 * r_stream._at(*o)[0] + r_stream._at(*o)[1] for o in order]
+    left_order = [blocks[o] for o in order]
+
+    def choose(b, values):
+        value = values[0]
+        for i in range(1, BLOCKS):
+            value = lax.select(b == i, values[i], value)
+        return value
+
+    sq_ref[...] = jnp.zeros_like(sq_ref)
+    out_ref[...] = jnp.zeros_like(out_ref)
+    half_rows = part(core * width, width, None)
+
     def factor_step(b, carry):
         r_stream.zero = l_stream.zero = b * 0
+
+        @pl.when(b == 2)
+        def _():
+            l_stream.relay_pair()
+            swap(0, 4)
+            swap(0, 5)
+
+        @pl.when(b == 3)
+        def _():
+            r_stream.relay_pair()
+
+        @pl.when(b == 6)
+        def _():
+            r_stream.end_own()
+            l_stream.end_own()
+            swap(0, 6)
+
+        @pl.when(b == 7)
+        def _():
+            r_stream.end_pair()
+            l_stream.end_pair()
+            swap(0, 7)
+
         at = pl.ds(pl.multiple_of(b * NB, NB), NB)
         y = inverse_factor(a_ref[at, at])
         linv_ref[at, at] = y
+        kr, kl = choose(b, right_order), choose(b, left_order)
+        sq_ref[...] += nn(b1t[kr], right[kr])
+        lhs = left[kl, half_rows, :]
+        out_ref[0:width, :] += nt(lhs, b1t[kl, 0:width, :])
+        out_ref[width:height, 0 : SPAN - width] += nt(lhs, b1t[kl, width:SPAN, :])
         below = lax.broadcasted_iota(jnp.int32, (SPAN, NB), 0) >= (b + 1) * NB
         panel = three(nt, split(a_ref[:, at]), split(y))
         panel = jnp.where(below, panel, 0.0)
@@ -403,56 +501,21 @@
 
         lax.fori_loop((b + 1) // 2, SPAN // tall, update, 0)
 
-        @pl.when(b == 1)
-        def _():
-            r_stream.relay_pair()
-
-        @pl.when(b == 2)
-        def _():
-            l_stream.send_pair()
-            swap(0, 1)
-            l_stream.relay_own()
-            swap(0, 2)
-            swap(0, 3)
-
-        @pl.when(b == 5)
-        def _():
-            l_stream.relay_pair()
-            swap(0, 4)
-            swap(0, 5)
-
         return carry
 
     lax.fori_loop(0, BLOCKS, factor_step, 0)
     r_stream.zero = l_stream.zero = 0
 
-    r_stream.end_own()
-    r_stream.end_pair()
-
-    def over_blocks(ref, tiles, rhs):
-        def step(k, carry):
-            def inner(tile, c):
-                value = rhs(k, at_tile(tile))
-
-                @pl.when(k == 0)
-                def _():
-                    ref[at_tile(tile), :] = value
-
-                @pl.when(k > 0)
-                def _():
-                    ref[at_tile(tile), :] += value
-
-                return c
-
-            return lax.fori_loop(0, tiles, inner, carry)
-
-        lax.fori_loop(0, 8, step, 0)
-
-    over_blocks(sq_ref, SPAN // rows, lambda k, at: nn(b1t[k, at, :], right[k]))
-    l_stream.end_own()
-    swap(0, 6)
-    l_stream.end_pair()
-    swap(0, 7)
+    first = row * height + core * width
+    for t in range(width // tall):
+        to = pl.ds(pl.multiple_of(core * width + t * tall, tall), tall)
+        for base, lo, hi in ((0, 0, width), (width, width, SPAN)):
+            shape = (tall, hi - lo)
+            srow = first + t * tall + lax.broadcasted_iota(jnp.int32, shape, 0)
+            scol = lo + lax.broadcasted_iota(jnp.int32, shape, 1)
+            strip = out_ref[base + t * tall : base + (t + 1) * tall, 0 : hi - lo]
+            strip += jnp.where(srow == scol, 1.0, 0.0)
+            sh_ref[to, lo:hi], sl_ref[to, lo:hi] = split(strip)
 
     size = NB
     while size < SPAN:
@@ -461,6 +524,13 @@
             inner = three(nn, split(a_ref[two, one]), split(linv_ref[one, one]))
             linv_ref[two, one] = -three(nn, split(linv_ref[two, two]), split(inner))
         size *= 2
+
+    def strips(side):
+        at = part(side * width, width, None)
+        return [single(14 + i, ref.at[at, :], other) for i, ref in enumerate((sh_ref, sl_ref))]
+
+    for copy in strips(core):
+        copy.start()
 
     cols = col * width + lax.broadcasted_iota(jnp.int32, (tall, width), 1)
     for b in range(SPAN // tall):
@@ -479,18 +549,25 @@
 
     for number in range(8):
         swapped(0, number)
-    over_blocks(out_ref, height // rows, lambda k, at: nn(left[k, at, :], right[k]))
-    over_blocks(sr_ref, height // rows, lambda k, at: nt(left[k, at, :], b1t[k]))
+
+    def over_rows(t, carry):
+        at = pl.ds(pl.multiple_of(t * tall, tall), tall)
+        value = nn(left[0, at, :], right[0])
+        for i in range(1, 8):
+            value += nn(left[i, at, :], right[i])
+        out_ref[at, :] = value
+        return carry
+
+    lax.fori_loop(0, height // tall, over_rows, 0)
+    for copy in strips(1 - core):
+        copy.wait_recv()
 
     def finish(t, carry):
         at = pl.ds(pl.multiple_of(t * tall, tall), tall)
         first = row * height + t * tall
         grow = first + lax.broadcasted_iota(jnp.int32, (tall, width), 0)
         gcol = col * width + lax.broadcasted_iota(jnp.int32, (tall, width), 1)
-        srow = first + lax.broadcasted_iota(jnp.int32, (tall, SPAN), 0)
-        scol = lax.broadcasted_iota(jnp.int32, (tall, SPAN), 1)
-        strip = split(sr_ref[at, :] + jnp.where(srow == scol, 1.0, 0.0))
-        value = three(nn, strip, (xh_ref[...], xl_ref[...]))
+        value = three(nn, (sh_ref[at, :], sl_ref[at, :]), (xh_ref[...], xl_ref[...]))
         system = out_ref[at, :] + jnp.where(grow == gcol, 1.0, 0.0)
         lead = jnp.where(grow >= gcol, value, 0.0)
         rest = jnp.where(grow < SPAN, 0.0, system - value)
@@ -503,6 +580,18 @@
         stream.drain()
     for base, number in swaps:
         swap_out(base, number).wait_send()
+
+    for copy in strips(core):
+        copy.wait_send()
+
+    for h in range(2):
+        @pl.when(moves_in)
+        def _(h=h):
+            along(h).wait_send()
+
+        @pl.when(moves_across)
+        def _(h=h):
+            over(h, row).wait_send()
 
     @pl.when(jnp.logical_and(seed, core == 0))
     def _():
@@ -543,16 +632,18 @@
             pltpu.VMEM((8, height, depth), bf16),
             pltpu.VMEM((8, depth, width), bf16),
             pltpu.VMEM((8, SPAN, depth), bf16),
+            pltpu.VMEM((width, depth), bf16),
             pltpu.VMEM((SPAN, SPAN), f32),
             pltpu.VMEM((SPAN, width), f32),
-            pltpu.VMEM((height, SPAN), f32),
+            pltpu.VMEM((height, SPAN), bf16),
+            pltpu.VMEM((height, SPAN), bf16),
             pltpu.VMEM((SPAN, SPAN), f32),
             pltpu.VMEM((SPAN, width), bf16),
             pltpu.VMEM((SPAN, width), bf16),
             dma((3, 9)), dma((3, 9)),
             dma((16,)), dma((16,)),
-            dma((10,)), dma((10,)),
-            dma((3,)),
+            dma((16,)), dma((16,)),
+            dma((5,)),
         ],
         compiler_params=pltpu.CompilerParams(
             collective_id=0, has_side_effects=True, vmem_limit_bytes=VMEM_LIMIT

time: 242 us -> 211 us (0.87)
  the two profiles are of different devices: /device:TPU:0 before, /device:TPU:39 now
where the time goes in v3:
time: 211 us
  Pallas kernels  203 us (96%)
  local copies, waits for them, and re-layouts  7.59 us (4%)
    pallas_call x1, Pallas kernels, whole(): pl.pallas_call(whole_kernel, out_shape=jax.ShapeDtypeStruct((height, widt...  203 us
    unnamed x6, local copies, waits for them, and re-layouts  6.33 us

profile of v3, /device:TPU:39, one launch (start us, length us, event | category | flops | bytes accessed | tf_op | source)
XLA Modules:
  0.0 211.2 jit_solution(8409026855788005100)
XLA Ops:
  0.0 0.8 dynamic-slice_convert_fusion
  0.8 0.1 copy.3
  0.9 0.1 broadcast_bitcast_fusion
  1.0 1.4 copy.4
  2.4 0.1 bitcast_multiply_fusion
  2.4 0.0 copy-start
  2.4 1.2 copy.5.m_ref
  3.6 0.0 copy-done
  3.6 202.7 %whole.1 = f32[1536,768]{1,0:T(8,128)} custom-call(bf16[512,768]{1,0:T(8,128)(2,1)} %copy.5.m_ref, bf16[768,512]{1,0:T(8,128)(2,1)} %bitcast.8), custom_call_target="tpu_custom_call" | custom-call | tf_op jit(solution)/shard_map/whole/pallas_call | solution.py:626
  206.3 4.8 %copy.8 = f32[1536,768]{1,0:T(8,128)} copy(f32[1536,768]{1,0:T(8,128)} %whole.1) | data formatting | bytes 9437184
  (1 shorter events, 0.0 us)
Async XLA Ops:
  2.4 1.2 copy-start

commit v4 on v3

--- a/solution.py
+++ b/solution.py
@@ -319,6 +319,7 @@
         pltpu.make_async_copy(mt_ref, stage, local.at[1]).start()
 
     own_right.wait()
+    r_stream.push(0, (0, 0), None, (0, 1))
     r_stream.push(1, (0, 0), None, (1, 0))
     r_stream.push(2, (0, 0), None, (-1, 0))
 
@@ -341,14 +342,6 @@
         single(9, chunk[1], over_col(2, yl)).start()
         single(6, chunk[0], over_col(0, yl)).wait_recv()
 
-    @pl.when(z == 2)
-    def _():
-        single(8, chunk[0], over_col(1, yl)).wait_recv()
-        single(9, chunk[1], over_col(3, yl)).wait_recv()
-
-    b_stream.send_own()
-    swap(8, 0)
-
     @pl.when(row == 0)
     def _():
         pltpu.make_async_copy(mt_ref, stage, local.at[1]).wait()
@@ -366,7 +359,13 @@
         def _(h=h):
             still(h).start()
 
-    r_stream.push(0, (0, 0), None, (0, 1))
+    @pl.when(z == 2)
+    def _():
+        single(8, chunk[0], over_col(1, yl)).wait_recv()
+        single(9, chunk[1], over_col(3, yl)).wait_recv()
+
+    b_stream.send_own()
+    swap(8, 0)
 
     rows = 512
 
@@ -390,10 +389,6 @@
 
     b_stream.send_pair()
     swap(8, 1)
-    b_stream.relay_own()
-    swap(8, 2)
-    swap(8, 3)
-
     for h in range(2):
         @pl.when(moves_across)
         def _(h=h):
@@ -405,13 +400,16 @@
 
     l_stream.send_own()
     swap(0, 0)
+    b_stream.relay_own()
+    swap(8, 2)
+    swap(8, 3)
     gram(0)
     gram(1)
     b_stream.relay_pair()
     swap(8, 4)
     swap(8, 5)
+    r_stream.relay_own()
     r_stream.send_pair()
-    r_stream.relay_own()
     gram(2)
     gram(3)
     l_stream.send_pair()
@@ -567,11 +565,18 @@
         first = row * height + t * tall
         grow = first + lax.broadcasted_iota(jnp.int32, (tall, width), 0)
         gcol = col * width + lax.broadcasted_iota(jnp.int32, (tall, width), 1)
-        value = three(nn, (sh_ref[at, :], sl_ref[at, :]), (xh_ref[...], xl_ref[...]))
+        value = nn(sh_ref[at, :], xh_ref[...]) + nn(sh_ref[at, :], xl_ref[...])
         system = out_ref[at, :] + jnp.where(grow == gcol, 1.0, 0.0)
         lead = jnp.where(grow >= gcol, value, 0.0)
         rest = jnp.where(grow < SPAN, 0.0, system - value)
         out_ref[at, :] = jnp.where(gcol < SPAN, lead, rest)
+
+        @pl.when(col < 2)
+        def _():
+            low = nn(sl_ref[at, :], xh_ref[...])
+            keep = jnp.logical_and(gcol < SPAN, grow >= gcol)
+            out_ref[at, :] += jnp.where(keep, low, 0.0)
+
         return carry
 
     lax.fori_loop(0, height // tall, finish, 0)

time: 211 us -> 195 us (0.924)
  the two profiles are of different devices: /device:TPU:39 before, /device:TPU:0 now
where the time goes in v4:
time: 195 us; the launch traced here: 194 us
  Pallas kernels  185 us (95%)
  local copies, waits for them, and re-layouts  7.59 us (4%)
    pallas_call x1, Pallas kernels, whole(): pl.pallas_call(whole_kernel, out_shape=jax.ShapeDtypeStruct((height, widt...  185 us
    unnamed x6, local copies, waits for them, and re-layouts  6.33 us

profile of v4, /device:TPU:0, one launch (start us, length us, event | category | flops | bytes accessed | tf_op | source)
XLA Modules:
  0.0 193.9 jit_solution(8561359433907448626)
XLA Ops:
  0.0 0.8 dynamic-slice_convert_fusion
  0.8 0.1 copy.3
  0.9 0.1 broadcast_bitcast_fusion
  1.0 1.4 copy.4
  2.4 0.1 bitcast_multiply_fusion
  2.4 0.0 copy-start
  2.4 1.2 copy.5.m_ref
  3.6 0.0 copy-done
  3.6 185.4 %whole.1 = f32[1536,768]{1,0:T(8,128)} custom-call(bf16[512,768]{1,0:T(8,128)(2,1)} %copy.5.m_ref, bf16[768,512]{1,0:T(8,128)(2,1)} %bitcast.8), custom_call_target="tpu_custom_call" | custom-call | tf_op jit(solution)/shard_map/whole/pallas_call | solution.py:631
  189.1 4.8 %copy.8 = f32[1536,768]{1,0:T(8,128)} copy(f32[1536,768]{1,0:T(8,128)} %whole.1) | data formatting | bytes 9437184
  (1 shorter events, 0.0 us)
Async XLA Ops:
  2.4 1.2 copy-start

commit v5 on v4

--- a/solution.py
+++ b/solution.py
@@ -153,9 +153,9 @@
 
 
 def whole_kernel(
-    m_ref, mt_ref, out_ref,
+    m_ref, mt_ref, result, out_ref,
     left, right, b1t, stage, a_ref, sq_ref, sh_ref, sl_ref, linv_ref, xh_ref, xl_ref,
-    send, recv, swap_send, swap_recv, one_send, one_recv, local,
+    send, recv, swap_send, swap_recv, one_send, one_recv, local, written,
 ):
     row, col = lax.axis_index("row"), lax.axis_index("col")
     x, yh = lax.div(row, 2), lax.rem(row, 2)
@@ -261,6 +261,30 @@
             def _(count=len(friends) + one + two):
                 pl.semaphore_wait(barrier, count)
 
+    def mine(h):
+        return part(core * width, width, h)
+
+    def along(h):
+        at = part(0, width, h)
+        return single(10 + h, mt_ref.at[at, :], inside, stage.at[at, :])
+
+    def over(h, slot):
+        return single(12 + h, stage.at[part(0, width, h), :], across, left.at[slot, mine(h), :])
+
+    def still(h):
+        return pltpu.make_async_copy(
+            stage.at[part(0, width, h), :], left.at[cross, mine(h), :], local.at[3 + h]
+        )
+
+    @pl.when(moves_in)
+    def _():
+        along(0).start()
+        along(1).start()
+
+    @pl.when(row == 0)
+    def _():
+        pltpu.make_async_copy(mt_ref, stage, local.at[1]).start()
+
     seed = jnp.logical_and(yl == 0, z == 0)
     spare = b1t.at[row, pl.ds(piece, width - piece), :]
     low = b1t.at[row, pl.ds(0, piece), :]
@@ -293,30 +317,6 @@
             single(2 + h, chunk[h], over_col(0, 1)).start()
             down(h)
             up(1 - h)
-
-    def mine(h):
-        return part(core * width, width, h)
-
-    def along(h):
-        at = part(0, width, h)
-        return single(10 + h, mt_ref.at[at, :], inside, stage.at[at, :])
-
-    def over(h, slot):
-        return single(12 + h, stage.at[part(0, width, h), :], across, left.at[slot, mine(h), :])
-
-    def still(h):
-        return pltpu.make_async_copy(
-            stage.at[part(0, width, h), :], left.at[cross, mine(h), :], local.at[3 + h]
-        )
-
-    @pl.when(moves_in)
-    def _():
-        along(0).start()
-        along(1).start()
-
-    @pl.when(row == 0)
-    def _():
-        pltpu.make_async_copy(mt_ref, stage, local.at[1]).start()
 
     own_right.wait()
     r_stream.push(0, (0, 0), None, (0, 1))
@@ -577,9 +577,15 @@
             keep = jnp.logical_and(gcol < SPAN, grow >= gcol)
             out_ref[at, :] += jnp.where(keep, low, 0.0)
 
+        pltpu.make_async_copy(out_ref.at[at, :], result.at[at, :], written.at[t]).start()
         return carry
 
     lax.fori_loop(0, height // tall, finish, 0)
+
+    def landed(t, carry):
+        at = pl.ds(pl.multiple_of(t * tall, tall), tall)
+        pltpu.make_async_copy(out_ref.at[at, :], result.at[at, :], written.at[t]).wait()
+        return carry
 
     for stream in (r_stream, b_stream, l_stream):
         stream.drain()
@@ -620,6 +626,8 @@
     @pl.when(z == 3)
     def _():
         single(9, chunk[1], over_col(2, yl)).wait_send()
+
+    lax.fori_loop(0, height // tall, landed, 0)
 
 
 def whole(masked, transposed):
@@ -627,13 +635,14 @@
     height = 2 * width
     f32, bf16 = jnp.float32, jnp.bfloat16
     dma = pltpu.SemaphoreType.DMA
-    hbm, vmem = pl.BlockSpec(memory_space=pl.ANY), pl.BlockSpec(memory_space=pltpu.VMEM)
+    hbm = pl.BlockSpec(memory_space=pl.ANY)
     return pl.pallas_call(
         whole_kernel,
         out_shape=jax.ShapeDtypeStruct((height, width), f32),
         in_specs=[hbm, hbm],
-        out_specs=vmem,
+        out_specs=hbm,
         scratch_shapes=[
+            pltpu.VMEM((height, width), f32),
             pltpu.VMEM((8, height, depth), bf16),
             pltpu.VMEM((8, depth, width), bf16),
             pltpu.VMEM((8, SPAN, depth), bf16),
@@ -649,6 +658,7 @@
             dma((16,)), dma((16,)),
             dma((16,)), dma((16,)),
             dma((5,)),
+            dma((height // TILE,)),
         ],
         compiler_params=pltpu.CompilerParams(
             collective_id=0, has_side_effects=True, vmem_limit_bytes=VMEM_LIMIT

time: 195 us -> 192 us (0.985)
  Pallas kernels: 185 us -> 182 us
    pallas_call x1, Pallas kernels: 185 us -> 182 us  [whole(): pl.pallas_call(whole_kernel, out_shape=jax.ShapeDtypeStruct((height, widt...]
where the time goes in v5:
time: 192 us; the launch traced here: 191 us
  Pallas kernels  182 us (95%)
  local copies, waits for them, and re-layouts  7.59 us (4%)
    pallas_call x1, Pallas kernels, whole(): pl.pallas_call(whole_kernel, out_shape=jax.ShapeDtypeStruct((height, widt...  182 us
    unnamed x6, local copies, waits for them, and re-layouts  6.33 us

profile of v5, /device:TPU:0, one launch (start us, length us, event | category | flops | bytes accessed | tf_op | source)
XLA Modules:
  0.0 190.6 jit_solution(7081774986142476250)
XLA Ops:
  0.0 0.8 dynamic-slice_convert_fusion
  0.8 0.1 copy.3
  0.9 0.1 broadcast_bitcast_fusion
  1.0 1.4 copy.4
  2.4 0.1 bitcast_multiply_fusion
  2.4 0.0 copy-start
  2.4 1.2 copy.5.m_ref
  3.6 0.0 copy-done
  3.6 182.2 %whole.1 = f32[1536,768]{1,0:T(8,128)} custom-call(bf16[512,768]{1,0:T(8,128)(2,1)} %copy.5.m_ref, bf16[768,512]{1,0:T(8,128)(2,1)} %bitcast.8), custom_call_target="tpu_custom_call" | custom-call | tf_op jit(solution)/shard_map/whole/pallas_call | solution.py:639
  185.8 4.8 %copy.8 = f32[1536,768]{1,0:T(8,128)} copy(f32[1536,768]{1,0:T(8,128)} %whole.1) | data formatting | bytes 9437184
  (1 shorter events, 0.0 us)
Async XLA Ops:
  2.4 1.2 copy-start

commit v6 on v5

--- a/solution.py
+++ b/solution.py
@@ -452,13 +452,13 @@
     def factor_step(b, carry):
         r_stream.zero = l_stream.zero = b * 0
 
-        @pl.when(b == 2)
+        @pl.when(b == 1)
         def _():
             l_stream.relay_pair()
             swap(0, 4)
             swap(0, 5)
 
-        @pl.when(b == 3)
+        @pl.when(b == 2)
         def _():
             r_stream.relay_pair()
 

time: 192 us -> 196 us (1.021)
  Pallas kernels: 182 us -> 188 us
    pallas_call x1, Pallas kernels: 182 us -> 188 us  [whole(): pl.pallas_call(whole_kernel, out_shape=jax.ShapeDtypeStruct((height, widt...]
where the time goes in v6:
time: 196 us
  Pallas kernels  188 us (96%)
  local copies, waits for them, and re-layouts  7.59 us (4%)
    pallas_call x1, Pallas kernels, whole(): pl.pallas_call(whole_kernel, out_shape=jax.ShapeDtypeStruct((height, widt...  188 us
    unnamed x6, local copies, waits for them, and re-layouts  6.33 us

profile of v6, /device:TPU:0, one launch (start us, length us, event | category | flops | bytes accessed | tf_op | source)
XLA Modules:
  0.0 196.0 jit_solution(3724359069153368328)
XLA Ops:
  0.0 0.8 dynamic-slice_convert_fusion
  0.8 0.1 copy.3
  0.9 0.1 broadcast_bitcast_fusion
  1.0 1.4 copy.4
  2.4 0.1 bitcast_multiply_fusion
  2.4 0.0 copy-start
  2.4 1.2 copy.5.m_ref
  3.6 0.0 copy-done
  3.6 187.6 %whole.1 = f32[1536,768]{1,0:T(8,128)} custom-call(bf16[512,768]{1,0:T(8,128)(2,1)} %copy.5.m_ref, bf16[768,512]{1,0:T(8,128)(2,1)} %bitcast.8), custom_call_target="tpu_custom_call" | custom-call | tf_op jit(solution)/shard_map/whole/pallas_call | solution.py:639
  191.2 4.8 %copy.8 = f32[1536,768]{1,0:T(8,128)} copy(f32[1536,768]{1,0:T(8,128)} %whole.1) | data formatting | bytes 9437184
  (1 shorter events, 0.0 us)
Async XLA Ops:
  2.4 1.2 copy-start
